TPU v7x, 8 devices: a whole 2x2x1 slice. The times are simulated.
8 devices in a mesh: batch: 1 (over z), stage: 2 (over y), seq: 4 (over x, core).
Axes of the slice: x: 2, y: 2, z: 1, core: 2. Of those that a mesh axis runs over, the one named last changes fastest.
Arguments:
- x_tokens: bfloat16 [2, 8192, 2048], P('batch', 'seq')
- norm_attn: bfloat16 [2, 2048], P('stage')
- w_query: bfloat16 [2, 2048, 1024], P('stage')
- w_key: bfloat16 [2, 2048, 1024], P('stage')
- w_value: bfloat16 [2, 2048, 2048], P('stage')
- w_gate: bfloat16 [2, 2048, 4], P('stage')
- gate_bias: float32 [2, 4], P('stage')
- norm_out: bfloat16 [2, 512], P('stage')
- w_out: bfloat16 [2, 2048, 2048], P('stage')
- norm_mlp: bfloat16 [2, 2048], P('stage')
- w_up: bfloat16 [2, 2048, 5632], P('stage')
- w_down: bfloat16 [2, 5632, 2048], P('stage')
Outputs:
- output 1: bfloat16 [2, 2, 8192, 2048], P('stage', 'batch', 'seq')
- output 2: float32 [2, 2, 4, 256, 512], P('stage', 'batch')
All inputs are finite; a program needn't handle non-finite values.
Results may differ from a plain program's by a relative error of at most 0.012754.
Values are sent between devices in bfloat16 or wider.
A program may use at most 1 GiB of HBM per device.

v0:
```python
import jax
import jax.numpy as jnp
from jax import lax
from jax.sharding import PartitionSpec as P

NORM_EPS = 1e-6


def rms_norm(values, gain_vec):
    mean_sq = jnp.mean(values * values, axis=-1, keepdims=True)
    return values * lax.rsqrt(mean_sq + NORM_EPS) * gain_vec.astype(jnp.float32)


def local_part(h_in, params):
    norm_attn, w_query, w_key, w_value, w_gate, gate_bias, norm_out, w_out, norm_mlp, w_up, w_down = params
    num_seqs, tok_len = h_in.shape[0], h_in.shape[1]
    num_heads = gate_bias.shape[0]
    key_dim = w_query.shape[1] // num_heads
    val_dim = norm_out.shape[0]
    h_f32 = h_in.astype(jnp.float32)
    u_norm = rms_norm(h_f32, norm_attn).astype(jnp.bfloat16)
    q_all = jnp.einsum('bcd,de->bce', u_norm, w_query, preferred_element_type=jnp.float32).astype(jnp.bfloat16)
    q_all = q_all.reshape(num_seqs, tok_len, num_heads, key_dim)
    k_raw = jnp.einsum('bcd,de->bce', u_norm, w_key, preferred_element_type=jnp.float32)
    k_all = (k_raw * key_dim ** -0.5).astype(jnp.bfloat16).reshape(num_seqs, tok_len, num_heads, key_dim)
    v_all = jnp.einsum('bcd,de->bce', u_norm, w_value, preferred_element_type=jnp.float32).astype(jnp.bfloat16)
    v_all = v_all.reshape(num_seqs, tok_len, num_heads, val_dim)
    gate_pre = jnp.einsum('bcd,dh->bch', u_norm, w_gate, preferred_element_type=jnp.float32) + gate_bias
    cum_decay = jnp.cumsum(jax.nn.log_sigmoid(gate_pre), axis=1)
    total_decay = cum_decay[:, -1, :]
    scores = jnp.einsum('bchk,bjhk->bhcj', q_all, k_all, preferred_element_type=jnp.float32)
    cum_heads = jnp.swapaxes(cum_decay, 1, 2)
    causal = jnp.arange(tok_len)[:, None] >= jnp.arange(tok_len)[None, :]
    decay_mat = jnp.exp(jnp.where(causal, cum_heads[:, :, :, None] - cum_heads[:, :, None, :], -jnp.inf))
    intra_out = jnp.einsum('bhcj,bjhv->bchv', scores * decay_mat, v_all, preferred_element_type=jnp.float32)
    k_decayed = k_all * jnp.exp(total_decay[:, None, :] - cum_decay)[..., None]
    local_state = jnp.einsum('bjhk,bjhv->bhkv', k_decayed, v_all, preferred_element_type=jnp.float32)
    return h_f32, q_all, cum_decay, total_decay, intra_out, local_state


def finish_part(h_f32, q_all, cum_decay, intra_out, state_in, params):
    norm_attn, w_query, w_key, w_value, w_gate, gate_bias, norm_out, w_out, norm_mlp, w_up, w_down = params
    num_seqs, tok_len = h_f32.shape[0], h_f32.shape[1]
    inter_out = jnp.einsum('bchk,bhkv->bchv', q_all, state_in, preferred_element_type=jnp.float32) * jnp.exp(cum_decay)[..., None]
    head_norm = rms_norm(inter_out + intra_out, norm_out).astype(jnp.bfloat16).reshape(num_seqs, tok_len, -1)
    h_mid = h_f32 + jnp.einsum('bce,ed->bcd', head_norm, w_out, preferred_element_type=jnp.float32)
    mlp_in = rms_norm(h_mid, norm_mlp).astype(jnp.bfloat16)
    hidden = jax.nn.gelu(jnp.einsum('bcd,df->bcf', mlp_in, w_up, preferred_element_type=jnp.float32), approximate=True).astype(jnp.bfloat16)
    return (h_mid + jnp.einsum('bcf,fd->bcd', hidden, w_down, preferred_element_type=jnp.float32)).astype(jnp.bfloat16)


def solution(mesh):
    num_stages = mesh.shape['stage']
    num_shards = mesh.shape['seq']
    step_count = num_stages + num_shards - 1
    stage_pairs = [(src_index, src_index + 1) for src_index in range(num_stages - 1)]
    seq_pairs = [(src_index, src_index + 1) for src_index in range(num_shards - 1)]
    mat_spec = P('stage', None, None)
    vec_spec = P('stage', None)
    weight_specs = (vec_spec, mat_spec, mat_spec, mat_spec, mat_spec, vec_spec, vec_spec, mat_spec, vec_spec, mat_spec, mat_spec)

    def device_program(x_tokens, norm_attn, w_query, w_key, w_value, w_gate, gate_bias, norm_out, w_out, norm_mlp, w_up, w_down):
        stage_idx = lax.axis_index('stage')
        seq_idx = lax.axis_index('seq')
        stacked = (norm_attn, w_query, w_key, w_value, w_gate, gate_bias, norm_out, w_out, norm_mlp, w_up, w_down)
        params = tuple(weight[0] for weight in stacked)
        num_seqs = x_tokens.shape[0]
        num_heads = gate_bias.shape[1]
        key_dim = w_query.shape[2] // num_heads
        val_dim = norm_out.shape[1]
        my_step = stage_idx + seq_idx

        def run_layer(operands):
            h_in, state_in = operands[0], operands[1]
            h_f32, q_all, cum_decay, total_decay, intra_out, local_state = local_part(h_in, params)
            state_out = jnp.exp(total_decay)[:, :, None, None] * state_in + local_state
            return finish_part(h_f32, q_all, cum_decay, intra_out, state_in, params), state_out

        def keep_layer(operands):
            return operands[2], operands[3]

        def step_body(step_num, loop_carry):
            h_recv, s_recv, y_done, s_done = loop_carry
            h_in = jnp.where(stage_idx == 0, x_tokens, h_recv)
            y_done, s_done = lax.cond(step_num == my_step, run_layer, keep_layer, (h_in, s_recv, y_done, s_done))
            h_recv = lax.ppermute(y_done, 'stage', stage_pairs)
            s_recv = lax.ppermute(s_done, 'seq', seq_pairs)
            return h_recv, s_recv, y_done, s_done

        zero_h = jnp.zeros_like(x_tokens)
        zero_s = jnp.zeros((num_seqs, num_heads, key_dim, val_dim), jnp.float32)
        loop_out = lax.fori_loop(0, step_count, step_body, (zero_h, zero_s, zero_h, zero_s))
        y_done, s_done = loop_out[2], loop_out[3]
        s_final = lax.psum(jnp.where(seq_idx == num_shards - 1, s_done, 0.0), 'seq')
        return y_done[None], s_final[None]

    return jax.shard_map(
        device_program,
        mesh=mesh,
        in_specs=(P('batch', 'seq', None),) + weight_specs,
        out_specs=(P('stage', 'batch', 'seq', None), P('stage', 'batch', None, None, None)),
        check_vma=False,
    )
```

profile of v0, /device:TPU:7, one launch (start us, length us, event | category | flops | bytes accessed | tf_op | source)
XLA Modules:
  0.0 3438.0 jit_solution(4697094696948128962)
XLA Ops:
  24.1 12.3 copy.83
  36.4 12.3 copy.85
  48.7 22.4 copy.86
  88.1 3253.4 %while.21 = (s32[]{:T(128)}, bf16[2,2048,2048]{1,2,0:T(8,128)(2,1)}, f32[2,4,256,512]{3,2,1,0:T(8,128)}, bf16[2,2048,2048]{1,2,0:T(8,128)(2,1)}, f32[2,4,256,512...) while((s32[]{:T(128)}, ...), condition=%wide.region_8.9_spmd, body=%wide.region_0.8_spmd.sunk | while | flops 352902643712 | bytes 1143456256 | solution.py:92
  105.0 352.3 %collective-permute-done = bf16[2,2048,2048]{1,2,0:T(8,128)(2,1)} collective-permute-done((bf16[2,2048,2048]{1,2,0:T(8,128)(2,1)}, bf16[2,2048,2048]{1,2,0:T(8,128)(2,1)}, u32[]{:S(2)}, u32[]{:S(2)}) %collective-permute-start) | collective-permute-done | bytes 16777248 | tf_op jit(solution)/shard_map/while/body/eval_jaxpr/ppermute | solution.py:86
  468.7 350.8 %collective-permute-done = bf16[2,2048,2048]{1,2,0:T(8,128)(2,1)} collective-permute-done((bf16[2,2048,2048]{1,2,0:T(8,128)(2,1)}, bf16[2,2048,2048]{1,2,0:T(8,128)(2,1)}, u32[]{:S(2)}, u32[]{:S(2)}) %collective-permute-start) | collective-permute-done | bytes 16777248 | tf_op jit(solution)/shard_map/while/body/eval_jaxpr/ppermute | solution.py:86
  822.2 9.5 collective-permute-done.1
  831.7 172.0 %collective-permute-done = bf16[2,2048,2048]{1,2,0:T(8,128)(2,1)} collective-permute-done((bf16[2,2048,2048]{1,2,0:T(8,128)(2,1)}, bf16[2,2048,2048]{1,2,0:T(8,128)(2,1)}, u32[]{:S(2)}, u32[]{:S(2)}) %collective-permute-start) | collective-permute-done | bytes 16777248 | tf_op jit(solution)/shard_map/while/body/eval_jaxpr/ppermute | solution.py:86
  1006.2 1581.5 %collective-permute-done.1 = f32[2,4,256,512]{3,2,1,0:T(8,128)} collective-permute-done((f32[2,4,256,512]{3,2,1,0:T(8,128)}, f32[2,4,256,512]{3,2,1,0:T(8,128)}, u32[]{:S(2)}, u32[]{:S(2)}) %collective-permute-start.1) | collective-permute-done | bytes 4194336 | tf_op jit(solution)/shard_map/while/body/eval_jaxpr/ppermute | solution.py:87
  2596.8 558.7 %conditional.2 = ((bf16[2,2048,2048]{1,2,0:T(8,128)(2,1)}, f32[2,4,256,512]{3,2,1,0:T(8,128)})) conditional(s32[]{:T(128)} %convert_element_type.89, (bf16[2,2048,2048]{1,2,0:T(8,128)(2,1)}, f32[2,4,256,512]{3,2,1,0:T(8,128)}) %tuple.56, (pred[]{:T(512)}, bf16[2,2048,2048]{1,2,0:T(8,128)(2,1)}, bf16[2,2048,2048]{1,2,0:T(8,128)(2,1)}, ...), branch_computations={%region_1.1_spmd, %region_2.7_spmd} | conditional | flops 352902643712 | bytes 1059569792 | solution.py:85
  2599.9 11.3 fusion.21
  2626.2 23.4 convolution_convert_fusion.1
  2649.5 23.4 multiply_convert_fusion.3
  2677.1 40.0 %convolution_convert_fusion = bf16[2,2048,2048]{1,2,0:T(8,128)(2,1)} fusion(bf16[2048,2048]{0,1:T(8,128)(2,1)S(1)} %bitcast.76, bf16[2,2048,2048]{1,2,0:T(8,128)(2,1)S(1)} %copy-done.1, f32[2048]{0:T(1024)S(1)} %convert_element_type.35, f32[2,2048]{1,0:T(2,128)S(1)} %add_rsqrt_fusion.2), kind=kOutput, calls=%fused_computation.44 | convolution fusion | flops 34401681408 | bytes 41967616 | tf_op jit(solution)/shard_map/while/body/eval_jaxpr/cond/branch_1_fun/bcd,de->bce/dot_general | solution.py:26
  2717.1 13.8 multiply_add_fusion
  2730.9 74.4 %fusion = f32[2,4,512,2048]{3,2,1,0:T(8,128)} fusion(bf16[2,2048,4,512]{1,3,2,0:T(8,128)(2,1)} %bitcast.85, f32[2,4,2048]{2,1,0:T(4,128)S(1)} %copy-done.6, pred[2048,2048]{1,0:T(8,128)(4,1)} %iota_compare_fusion, bf16[2,2048,4,256]{1,3,2,0:T(8,128)(2,1)} %bitcast.71, bf16[2,2048,4,256]{1,3,2,0:T(8,128)(2,1)} %bitcast.87), kind=kOutput, calls=%fused_computation.1 | convolution fusion | flops 51640270848 | bytes 71368704 | tf_op jit(solution)/shard_map/while/body/eval_jaxpr/cond/branch_1_fun/bhcj,bjhv->bchv/dot_general | solution.py:35
  2805.3 25.6 multiply_reduce_fusion.1
  2831.0 21.2 multiply_convert_fusion.1
  2854.8 43.6 %multiply_reduce_fusion = (f32[2,2048]{1,0:T(2,128)S(1)}, f32[2,2048,2048]{1,2,0:T(8,128)}) fusion(bf16[2,2048,2048]{1,2,0:T(8,128)(2,1)} %bitcast.70, bf16[2048,2048]{0,1:T(8,128)(2,1)S(1)} %copy-done.4, bf16[2,2048,2048]{1,2,0:T(8,128)(2,1)S(1)} %copy-done.2), kind=kOutput, calls=%fused_computation.30 | convolution fusion | flops 34393288704 | bytes 75513856 | tf_op jit(solution)/shard_map/while/body/eval_jaxpr/cond/branch_1_fun/bce,ed->bcd/dot_general | solution.py:46
  2898.4 111.5 %fusion.25 = f32[2,2048,5632]{2,1,0:T(8,128)} fusion(bf16[2048,5632]{1,0:T(8,128)(2,1)} %get-tuple-element.458, f32[2,2048,2048]{1,2,0:T(8,128)} %get-tuple-element.609, f32[2048]{0:T(1024)S(1)} %copy-done.9, f32[2,2048]{1,0:T(2,128)S(1)} %add_rsqrt_fusion.1), kind=kOutput, calls=%fused_computation.34 | convolution fusion | flops 94514446336 | bytes 148922368 | tf_op jit(solution)/shard_map/while/body/eval_jaxpr/cond/branch_1_fun/bcd,df->bcf/dot_general | solution.py:48
  3009.9 145.3 %add_convert_fusion = bf16[2,2048,2048]{1,2,0:T(8,128)(2,1)} fusion(f32[2,2048,2048]{1,2,0:T(8,128)} %get-tuple-element.609, bf16[5632,2048]{1,0:T(8,128)(2,1)} %get-tuple-element.459, f32[2,2048,5632]{2,1,0:T(8,128)} %fusion.25), kind=kOutput, calls=%fused_computation.28 | convolution fusion | flops 94713675776 | bytes 165675008 | tf_op jit(solution)/shard_map/while/body/eval_jaxpr/cond/branch_1_fun/bcf,fd->bcd/dot_general | solution.py:49
  3165.8 173.8 %collective-permute-done = bf16[2,2048,2048]{1,2,0:T(8,128)(2,1)} collective-permute-done((bf16[2,2048,2048]{1,2,0:T(8,128)(2,1)}, bf16[2,2048,2048]{1,2,0:T(8,128)(2,1)}, u32[]{:S(2)}, u32[]{:S(2)}) %collective-permute-start) | collective-permute-done | bytes 16777248 | tf_op jit(solution)/shard_map/while/body/eval_jaxpr/ppermute | solution.py:86
  3346.5 22.4 copy.87
  3368.9 57.1 %all-reduce.2.cloned.1.call-done = f32[1,2,4,256,512]{4,3,2,1,0:T(8,128)} async-done(((f32[1,2,4,256,512]{4,3,2,1,0:T(8,128)}), f32[1,2,4,256,512]{4,3,2,1,0:T(8,128)}) %all-reduce.2.cloned.1.call-update) | async-done | bytes 4194320 | tf_op jit(solution)/shard_map/psum | solution.py:94
  (75 shorter events, 121.0 us)
Async XLA Ops:
  7.2 3418.8 %all-reduce.2.cloned.1.call-start = ((), (), s32[]{:S(2)}) async-start(), calls=%async_computation | async-start | bytes 8388608 | tf_op jit(solution)/shard_map/psum | solution.py:94
  94.4 363.0 %collective-permute-start = (bf16[2,2048,2048]{1,2,0:T(8,128)(2,1)}, bf16[2,2048,2048]{1,2,0:T(8,128)(2,1)}, u32[]{:S(2)}, u32[]{:S(2)}) collective-permute-start(bf16[2,2048,2048]{1,2,0:T(8,128)(2,1)} %get-tuple-element.776), channel_id=1, source_target_pairs={{0,4},{1,5},{2,6},{3,7}} | collective-permute-start | bytes 50331656 | tf_op jit(solution)/shard_map/while/body/eval_jaxpr/ppermute | solution.py:86
  95.7 9.3 collective-permute-start.1
  457.4 362.2 %collective-permute-start = (bf16[2,2048,2048]{1,2,0:T(8,128)(2,1)}, bf16[2,2048,2048]{1,2,0:T(8,128)(2,1)}, u32[]{:S(2)}, u32[]{:S(2)}) collective-permute-start(bf16[2,2048,2048]{1,2,0:T(8,128)(2,1)} %get-tuple-element.776), channel_id=1, source_target_pairs={{0,4},{1,5},{2,6},{3,7}} | collective-permute-start | bytes 50331656 | tf_op jit(solution)/shard_map/while/body/eval_jaxpr/ppermute | solution.py:86
  458.7 10.1 collective-permute-start.1
  819.6 184.1 %collective-permute-start = (bf16[2,2048,2048]{1,2,0:T(8,128)(2,1)}, bf16[2,2048,2048]{1,2,0:T(8,128)(2,1)}, u32[]{:S(2)}, u32[]{:S(2)}) collective-permute-start(bf16[2,2048,2048]{1,2,0:T(8,128)(2,1)} %get-tuple-element.776), channel_id=1, source_target_pairs={{0,4},{1,5},{2,6},{3,7}} | collective-permute-start | bytes 50331656 | tf_op jit(solution)/shard_map/while/body/eval_jaxpr/ppermute | solution.py:86
  820.9 10.8 collective-permute-start.1
  1003.7 1593.1 %collective-permute-start = (bf16[2,2048,2048]{1,2,0:T(8,128)(2,1)}, bf16[2,2048,2048]{1,2,0:T(8,128)(2,1)}, u32[]{:S(2)}, u32[]{:S(2)}) collective-permute-start(bf16[2,2048,2048]{1,2,0:T(8,128)(2,1)} %get-tuple-element.776), channel_id=1, source_target_pairs={{0,4},{1,5},{2,6},{3,7}} | collective-permute-start | bytes 50331656 | tf_op jit(solution)/shard_map/while/body/eval_jaxpr/ppermute | solution.py:86
  1004.9 1582.8 %collective-permute-start.1 = (f32[2,4,256,512]{3,2,1,0:T(8,128)}, f32[2,4,256,512]{3,2,1,0:T(8,128)}, u32[]{:S(2)}, u32[]{:S(2)}) collective-permute-start(f32[2,4,256,512]{3,2,1,0:T(8,128)} %get-tuple-element.777), channel_id=1, source_target_pairs={{0,1},{1,2},{2,3},{4,5},{5,6},{6,7}} | collective-permute-start | bytes 12582920 | tf_op jit(solution)/shard_map/while/body/eval_jaxpr/ppermute | solution.py:87
  2611.2 5.7 copy-start
  2624.7 24.8 copy-start.5
  2626.1 23.4 copy-start.1
  2626.2 50.9 %slice-start = ((s8[8388608]{0:T(1024)(128)(4,1)}), s8[4194304]{0:T(1024)(128)(4,1)S(1)}, s32[]{:S(2)}) async-start(s8[8388608]{0:T(1024)(128)(4,1)} %bitcast.75), calls=%async_computation.1 | async-start | bytes 8388608 | tf_op jit(solution)/shard_map/while/body/eval_jaxpr/cond
  2649.5 27.5 slice-start.1
  2677.0 40.0 %copy-start.7 = (f32[2,2048,4]{1,2,0:T(4,128)S(1)}, f32[2,2048,4]{1,2,0:T(4,128)}, u32[]{:S(2)}) copy-start(f32[2,2048,4]{1,2,0:T(4,128)} %get-tuple-element.604) | copy-start | bytes 196612 | tf_op jit(solution)/shard_map/while/body/eval_jaxpr/cond
  2677.0 40.0 %copy-start.10 = (f32[2,4]{1,0:T(2,128)S(1)}, f32[2,4]{1,0:T(2,128)}, u32[]{:S(2)}) copy-start(f32[2,4]{1,0:T(2,128)} %exp.20) | copy-start | bytes 100 | tf_op jit(solution)/shard_map/while/body/eval_jaxpr/cond
  2717.1 13.8 copy-start.6
  2730.9 74.4 %copy-start.3 = (f32[2,2048,4]{1,2,0:T(4,128)S(1)}, f32[2,2048,4]{1,2,0:T(4,128)}, u32[]{:S(2)}) copy-start(f32[2,2048,4]{1,2,0:T(4,128)} %get-tuple-element.605) | copy-start | bytes 196612 | tf_op jit(solution)/shard_map/while/body/eval_jaxpr/cond
  2805.3 25.6 copy-start.8
  2830.9 21.2 copy-start.2
  2831.0 23.8 copy-start.4
  2854.8 43.6 %copy-start.9 = (f32[2048]{0:T(1024)S(1)}, f32[2048]{0:T(1024)}, u32[]{:S(2)}) copy-start(f32[2048]{0:T(1024)} %convert_element_type.42) | copy-start | bytes 24580 | tf_op jit(solution)/shard_map/while/body/eval_jaxpr/cond
  3155.4 184.1 %collective-permute-start = (bf16[2,2048,2048]{1,2,0:T(8,128)(2,1)}, bf16[2,2048,2048]{1,2,0:T(8,128)(2,1)}, u32[]{:S(2)}, u32[]{:S(2)}) collective-permute-start(bf16[2,2048,2048]{1,2,0:T(8,128)(2,1)} %get-tuple-element.776), channel_id=1, source_target_pairs={{0,4},{1,5},{2,6},{3,7}} | collective-permute-start | bytes 50331656 | tf_op jit(solution)/shard_map/while/body/eval_jaxpr/ppermute | solution.py:86
  3156.7 9.0 collective-permute-start.1
Sparse Core Ops, SparseCore 0:
  3346.6 79.2 all-reduce.1
where the time goes:
time: 3450 us; the launch traced here: 3440 us
  waiting for transfers between devices  2730 us (79%)
  matrix products  506 us (15%)
  local copies, waits for them, and re-layouts  113 us (3%)
  other arithmetic  52 us (2%)
    ppermute x5, waiting for transfers between devices, step_body(): s_recv = lax.ppermute(s_done, 'seq', seq_pairs)  1620 us
    ppermute x5, waiting for transfers between devices, step_body(): h_recv = lax.ppermute(y_done, 'stage', stage_pairs)  1060 us
    dot_general x1, matrix products, finish_part(): jnp.einsum('bcf,fd->bcd', hidden, w_down, preferred_element_type=jnp.floa...  145 us
    dot_general x1, matrix products, finish_part(): jnp.einsum('bcd,df->bcf', mlp_in, w_up, preferred_element_type=jnp.float32)  112 us
    dot_general x1, matrix products, local_part(): jnp.einsum('bhcj,bjhv->bchv', scores * decay_mat, v_all, preferred_elemen...  74.4 us
  transfers between devices with their start and end apart: 11, of which 11 were waited for; matrix products, arithmetic and copies ran while one was open for 1% of the time, Pallas kernels for 0%

commit v1 on v0

v1 whole, which is shorter than its diff:
```python
import functools

import jax
import jax.numpy as jnp
from jax import lax
from jax.experimental import pallas as pl
from jax.experimental.pallas import tpu as pltpu
from jax.sharding import PartitionSpec as P

NORM_EPS = 1e-6
MESH = pl.DeviceIdType.MESH
BF16 = jnp.bfloat16
F32 = jnp.float32
NUM_W = 5
NUM_W2 = 3
AHEAD = 2


def mean_sq_scale(values):
    return lax.rsqrt(jnp.mean(values * values, axis=-1, keepdims=True) + NORM_EPS)


def dot32(lhs, rhs):
    return jnp.dot(lhs, rhs, preferred_element_type=F32)


def layer_kernel(
    rows, heads, tile, tile2,
    x, wq, wk, wv, wo, w1, w2, wa, beta, g1, go, g2,
    y_out, s_out, xbuf, hbuf,
    wqkv, wbuf, w2buf, hin, u, qb, kb, vb, ob, r, hid, ybuf, state, s_in, l_own, l_recv, cum, cum_t,
    wqkv_sem, w_sem, w2_sem, hin_sem, x_send, x_recv, h_send, h_recv, y_send, y_recv, l_send_sem, l_recv_sem, s_sem, s_recv_sem,
):
    stage = lax.axis_index('stage')
    me = lax.axis_index('seq')
    chip = lax.div(me, 2)
    core = lax.rem(me, 2)
    depth = x.shape[2]
    key_dim = wq.shape[1] // heads
    val_dim = wv.shape[1] // heads
    keys = heads * key_dim
    per_home = x.shape[1] // (2 * rows)
    chunks = 4 * per_home
    q_tiles = wq.shape[1] // tile
    v_tiles = wv.shape[1] // tile
    proj_tiles = 2 * q_tiles + v_tiles
    o_tiles = depth // tile
    up_tiles = w1.shape[1] // tile
    w_tiles = o_tiles + up_tiles
    down_tiles = depth // tile2
    last = chunks - 1

    def at(stage_pos, seq_pos):
        return {'stage': stage_pos, 'seq': seq_pos}

    def span(chunk, core_pos):
        return pl.ds(pl.multiple_of((lax.rem(chunk, per_home) * 2 + core_pos) * rows, rows), rows)

    def proj_copies():
        copies = []
        for i in range(q_tiles):
            copies.append(pltpu.make_async_copy(wk.at[:, pl.ds(i * tile, tile)], wqkv.at[i], wqkv_sem.at[i]))
        for i in range(v_tiles):
            n = q_tiles + i
            copies.append(pltpu.make_async_copy(wv.at[:, pl.ds(i * tile, tile)], wqkv.at[n], wqkv_sem.at[n]))
        for i in range(q_tiles):
            n = q_tiles + v_tiles + i
            copies.append(pltpu.make_async_copy(wq.at[:, pl.ds(i * tile, tile)], wqkv.at[n], wqkv_sem.at[n]))
        return copies

    def start_w(i):
        slot = lax.rem(i, NUM_W)

        @pl.when(i < o_tiles)
        def _():
            col = pl.ds(pl.multiple_of(i * tile, tile), tile)
            pltpu.make_async_copy(wo.at[:, col], wbuf.at[slot], w_sem.at[slot]).start()

        @pl.when(i >= o_tiles)
        def _():
            col = pl.ds(pl.multiple_of((i - o_tiles) * tile, tile), tile)
            pltpu.make_async_copy(w1.at[:, col], wbuf.at[slot], w_sem.at[slot]).start()

    def wait_w(i):
        slot = lax.rem(i, NUM_W)
        pltpu.make_async_copy(w1.at[:, pl.ds(0, tile)], wbuf.at[slot], w_sem.at[slot]).wait()
        return slot

    def next_w(chunk, i):
        @pl.when((chunk < last) | (i + NUM_W < w_tiles))
        def _():
            start_w(lax.rem(i + NUM_W, w_tiles))

    def w2_copy(n, slot):
        col = pl.ds(pl.multiple_of(n * tile2, tile2), tile2)
        return pltpu.make_async_copy(w2.at[:, col], w2buf.at[slot], w2_sem.at[slot])

    def x_copy(chunk, dest):
        return pltpu.make_async_remote_copy(
            src_ref=x.at[dest // 2, span(chunk, dest % 2)],
            dst_ref=xbuf.at[chunk],
            send_sem=x_send.at[lax.rem(chunk, per_home), dest],
            recv_sem=x_recv.at[chunk],
            device_id=at(0, dest),
            device_id_type=MESH,
        )

    def x_mine(chunk, dest):
        home = lax.div(chunk, per_home)
        same = lax.div(home, 2) == dest // 2
        return (me == home) & (home != dest) & ((same & (stage == 0)) | ((lax.div(home, 2) != dest // 2) & (stage == dest % 2)))

    def push_x(chunk):
        for dest in range(4):
            @pl.when(x_mine(chunk, dest))
            def _():
                x_copy(chunk, dest).start()

    def landed(buf, sem, chunk):
        pltpu.make_async_remote_copy(
            src_ref=buf.at[chunk], dst_ref=buf.at[chunk], send_sem=x_send.at[0, 0], recv_sem=sem.at[chunk],
            device_id=at(stage, me), device_id_type=MESH,
        ).wait_recv()

    def load_h(chunk):
        slot = lax.rem(chunk, 2)
        local = me == lax.div(chunk, per_home)

        @pl.when((stage == 0) & local)
        def _():
            pltpu.make_async_copy(x.at[chip, span(chunk, core)], hin.at[slot], hin_sem.at[slot]).start()

        @pl.when((stage == 0) & (me != lax.div(chunk, per_home)))
        def _():
            landed(xbuf, x_recv, chunk)
            pltpu.make_async_copy(xbuf.at[chunk], hin.at[slot], hin_sem.at[slot]).start()

        @pl.when(stage == 1)
        def _():
            landed(hbuf, h_recv, chunk)
            pltpu.make_async_copy(hbuf.at[chunk], hin.at[slot], hin_sem.at[slot]).start()

    def h_copy(chunk):
        slot = lax.rem(chunk, 2)
        return pltpu.make_async_remote_copy(
            src_ref=ybuf.at[slot], dst_ref=hbuf.at[chunk], send_sem=h_send.at[slot], recv_sem=h_recv.at[chunk],
            device_id=at(1, me), device_id_type=MESH,
        )

    def y_local(chunk):
        slot = lax.rem(chunk, 2)
        return pltpu.make_async_copy(ybuf.at[slot], y_out.at[chip, span(chunk, core)], y_send.at[slot])

    def y_remote(chunk):
        slot = lax.rem(chunk, 2)
        return pltpu.make_async_remote_copy(
            src_ref=ybuf.at[slot], dst_ref=y_out.at[chip, span(chunk, core)], send_sem=y_send.at[slot],
            recv_sem=y_recv.at[lax.rem(chunk, per_home), me],
            device_id=at(stage, lax.div(chunk, per_home)), device_id_type=MESH,
        )

    def send_y(chunk):
        @pl.when(stage == 0)
        def _():
            h_copy(chunk).start()

        @pl.when(me == lax.div(chunk, per_home))
        def _():
            y_local(chunk).start()

        @pl.when(me != lax.div(chunk, per_home))
        def _():
            y_remote(chunk).start()

    def sent_y(chunk):
        @pl.when(stage == 0)
        def _():
            h_copy(chunk).wait_send()

        @pl.when(me == lax.div(chunk, per_home))
        def _():
            y_local(chunk).wait()

        @pl.when(me != lax.div(chunk, per_home))
        def _():
            y_remote(chunk).wait_send()

    def l_copy(chunk):
        slot = lax.rem(chunk, 2)
        return pltpu.make_async_remote_copy(
            src_ref=l_own, dst_ref=l_recv.at[slot], send_sem=l_send_sem, recv_sem=l_recv_sem.at[slot],
            device_id=at(stage, chip * 2 + 1 - core), device_id_type=MESH,
        )

    def s_local():
        return pltpu.make_async_copy(state, s_out.at[chip], s_sem.at[0])

    def s_remote():
        return pltpu.make_async_remote_copy(
            src_ref=state, dst_ref=s_out.at[chip], send_sem=s_sem.at[1], recv_sem=s_recv_sem,
            device_id=at(stage, (1 - chip) * 2 + core), device_id_type=MESH,
        )

    barrier = pltpu.get_barrier_semaphore()
    for stage_pos in range(2):
        for seq_pos in range(4):
            pl.semaphore_signal(barrier, inc=1, device_id=at(stage_pos, seq_pos), device_id_type=MESH)
    pl.semaphore_wait(barrier, 8)

    for chunk in range(AHEAD):
        push_x(jnp.int32(chunk))
    first_copies = proj_copies()
    for copy in first_copies:
        copy.start()
    for i in range(NUM_W):
        start_w(jnp.int32(i))
    for n in range(NUM_W2):
        w2_copy(n, n).start()
    state[...] = jnp.zeros_like(state)
    load_h(jnp.int32(0))
    for copy in first_copies:
        copy.wait()

    def project(i, carry):
        prod = dot32(u[...], wqkv[i])

        @pl.when(i < q_tiles)
        def _():
            scaled = (prod * key_dim ** -0.5).astype(BF16)
            kb[2 * i] = scaled[:, :key_dim]
            kb[2 * i + 1] = scaled[:, key_dim:]

        @pl.when((i >= q_tiles) & (i < q_tiles + v_tiles))
        def _():
            vb[i - q_tiles] = prod.astype(BF16)

        @pl.when(i >= q_tiles + v_tiles)
        def _():
            got = prod.astype(BF16)
            qb[2 * (i - q_tiles - v_tiles)] = got[:, :key_dim]
            qb[2 * (i - q_tiles - v_tiles) + 1] = got[:, key_dim:]

        return carry

    def chunk_body(chunk, carry):
        slot = lax.rem(chunk, 2)

        @pl.when(chunk + AHEAD < chunks)
        def _():
            push_x(chunk + AHEAD)

        pltpu.make_async_copy(hbuf.at[0], hin.at[slot], hin_sem.at[slot]).wait()
        h_f32 = hin[slot].astype(F32)
        u[...] = (h_f32 * mean_sq_scale(h_f32) * g1[...]).astype(BF16)

        gate = dot32(u[...], wa[...]) + beta[...]
        log_decay = jnp.minimum(gate, 0.0) - jnp.log1p(jnp.exp(-jnp.abs(gate)))
        row_id = lax.broadcasted_iota(jnp.int32, (rows, rows), 0)
        col_id = lax.broadcasted_iota(jnp.int32, (rows, rows), 1)
        tril = (row_id >= col_id).astype(F32)
        cum_val = jnp.dot(tril, log_decay, precision=lax.Precision.HIGHEST, preferred_element_type=F32)
        cum[...] = cum_val
        cum_t[...] = cum_val.T

        lax.fori_loop(0, q_tiles + v_tiles, project, 0)
        for h in range(heads):
            ci = cum[:, h:h + 1]
            total = cum[rows - 1:rows, h:h + 1]
            kd = (kb[h].astype(F32) * jnp.exp(total - ci)).astype(BF16)
            l_own[h * key_dim:(h + 1) * key_dim, :] = lax.dot_general(
                kd, vb[h], (((0,), (0,)), ((), ())), preferred_element_type=F32)
        last_row = cum_t[:, rows - 1:rows]
        l_own[keys:keys + 8, :] = jnp.broadcast_to(jnp.exp(last_row[:8]), (8, val_dim))
        l_copy(chunk).start()

        lax.fori_loop(q_tiles + v_tiles, proj_tiles, project, 0)
        for h in range(heads):
            ci = cum[:, h:h + 1]
            cj = cum_t[h:h + 1, :]
            scores = lax.dot_general(qb[h], kb[h], (((1,), (1,)), ((), ())), preferred_element_type=F32)
            decay = jnp.exp(jnp.where(row_id >= col_id, ci - cj, -jnp.inf))
            r[:, h * val_dim:(h + 1) * val_dim] = dot32((scores * decay).astype(BF16), vb[h])

        l_copy(chunk).wait_send()
        l_copy(chunk).wait_recv()

        def update(h, mine, theirs):
            rng = slice(h * key_dim, (h + 1) * key_dim)
            row = slice(keys + h, keys + h + 1)
            mid = state[rng] * l_recv[slot, row] + l_recv[slot, rng]
            return mid

        @pl.when(core == 0)
        def _():
            for h in range(heads):
                rng = slice(h * key_dim, (h + 1) * key_dim)
                row = slice(keys + h, keys + h + 1)
                prev = state[rng]
                s_in[rng] = prev.astype(BF16)
                mid = prev * l_own[row] + l_own[rng]
                state[rng] = mid * l_recv[slot, row] + l_recv[slot, rng]

        @pl.when(core == 1)
        def _():
            for h in range(heads):
                rng = slice(h * key_dim, (h + 1) * key_dim)
                row = slice(keys + h, keys + h + 1)
                mid = state[rng] * l_recv[slot, row] + l_recv[slot, rng]
                s_in[rng] = mid.astype(BF16)
                state[rng] = mid * l_own[row] + l_own[rng]

        @pl.when(chunk == last)
        def _():
            s_local().start()
            s_remote().start()

        for h in range(heads):
            col = slice(h * val_dim, (h + 1) * val_dim)
            inter = dot32(qb[h], s_in[h * key_dim:(h + 1) * key_dim])
            o_val = r[:, col] + inter * jnp.exp(cum[:, h:h + 1])
            ob[:, col] = (o_val * mean_sq_scale(o_val) * go[...]).astype(BF16)

        def out_proj(i, carry):
            wslot = wait_w(i)
            col = pl.ds(pl.multiple_of(i * tile, tile), tile)
            r[:, col] = hin[slot, :, col].astype(F32) + dot32(ob[...], wbuf[wslot])
            next_w(chunk, i)
            return carry

        lax.fori_loop(0, o_tiles, out_proj, 0)
        r_val = r[...]
        u[...] = (r_val * mean_sq_scale(r_val) * g2[...]).astype(BF16)

        def up(f, carry):
            i = f + o_tiles
            wslot = wait_w(i)
            for part in range(2):
                half = tile // 2
                prod = dot32(u[...], wbuf[wslot, :, part * half:(part + 1) * half])
                hid[:, pl.ds(pl.multiple_of(f * tile + part * half, half), half)] = jax.nn.gelu(prod, approximate=True).astype(BF16)
            next_w(chunk, i)
            return carry

        lax.fori_loop(0, up_tiles, up, 0)

        @pl.when(chunk >= 2)
        def _():
            sent_y(chunk - 2)

        def down(n, carry):
            g = chunk * down_tiles + n
            wslot = lax.rem(g, NUM_W2)
            w2_copy(n, wslot).wait()
            col = pl.ds(pl.multiple_of(n * tile2, tile2), tile2)
            ybuf[slot, :, col] = (r[:, col] + dot32(hid[...], w2buf[wslot])).astype(BF16)

            @pl.when((chunk < last) | (n + NUM_W2 < down_tiles))
            def _():
                w2_copy(lax.rem(n + NUM_W2, down_tiles), wslot).start()

            @pl.when((chunk < last) & (n == down_tiles - 2))
            def _():
                load_h(chunk + 1)

            return carry

        lax.fori_loop(0, down_tiles, down, 0)
        send_y(chunk)
        return carry

    lax.fori_loop(0, chunks, chunk_body, 0)

    sent_y(jnp.int32(chunks - 2))
    sent_y(jnp.int32(chunks - 1))
    s_local().wait()
    s_remote().wait_send()
    pltpu.make_async_remote_copy(
        src_ref=state, dst_ref=s_out.at[1 - chip], send_sem=s_sem.at[1], recv_sem=s_recv_sem,
        device_id=at(stage, me), device_id_type=MESH,
    ).wait_recv()

    def x_done(chunk, carry):
        for dest in range(4):
            @pl.when(x_mine(chunk, dest))
            def _():
                x_copy(chunk, dest).wait_send()
        return carry

    lax.fori_loop(0, chunks, x_done, 0)

    def y_done(e, carry):
        for src in range(4):
            @pl.when(me != src)
            def _():
                pltpu.make_async_remote_copy(
                    src_ref=ybuf.at[0], dst_ref=y_out.at[src // 2, span(e, src % 2)], send_sem=y_send.at[0],
                    recv_sem=y_recv.at[e, src], device_id=at(stage, me), device_id_type=MESH,
                ).wait_recv()
        return carry

    lax.fori_loop(0, per_home, y_done, 0)


def run_layers(rows, tile, tile2, x, wq, wk, wv, wo, w1, w2, wa, beta, g1, go, g2, heads):
    seqs, tok_len, depth = x.shape
    keys, values, ffn = wq.shape[1], wv.shape[1], w1.shape[1]
    key_dim, val_dim = keys // heads, values // heads
    per_home = tok_len // (2 * rows)
    chunks = 4 * per_home
    proj_tiles = (2 * keys + values) // tile
    hbm = pl.BlockSpec(memory_space=pl.ANY)
    vmem = pl.BlockSpec(memory_space=pltpu.VMEM)
    dma = pltpu.SemaphoreType.DMA
    outs = pl.pallas_call(
        functools.partial(layer_kernel, rows, heads, tile, tile2),
        out_shape=(
            jax.ShapeDtypeStruct((seqs, tok_len, depth), BF16),
            jax.ShapeDtypeStruct((seqs, keys, val_dim), F32),
            jax.ShapeDtypeStruct((chunks, rows, depth), BF16),
            jax.ShapeDtypeStruct((chunks, rows, depth), BF16),
        ),
        in_specs=[hbm] * 7 + [vmem] * 5,
        out_specs=(hbm, hbm, hbm, hbm),
        scratch_shapes=[
            pltpu.VMEM((proj_tiles, depth, tile), BF16),
            pltpu.VMEM((NUM_W, depth, tile), BF16),
            pltpu.VMEM((NUM_W2, ffn, tile2), BF16),
            pltpu.VMEM((2, rows, depth), BF16),
            pltpu.VMEM((rows, depth), BF16),
            pltpu.VMEM((heads, rows, key_dim), BF16),
            pltpu.VMEM((heads, rows, key_dim), BF16),
            pltpu.VMEM((heads, rows, val_dim), BF16),
            pltpu.VMEM((rows, values), BF16),
            pltpu.VMEM((rows, depth), F32),
            pltpu.VMEM((rows, ffn), BF16),
            pltpu.VMEM((2, rows, depth), BF16),
            pltpu.VMEM((keys, val_dim), F32),
            pltpu.VMEM((keys, val_dim), BF16),
            pltpu.VMEM((keys + 8, val_dim), F32),
            pltpu.VMEM((2, keys + 8, val_dim), F32),
            pltpu.VMEM((rows, 128), F32),
            pltpu.VMEM((128, rows), F32),
            dma((proj_tiles,)), dma((NUM_W,)), dma((NUM_W2,)), dma((2,)),
            dma((per_home, 4)), dma((chunks,)), dma((2,)), dma((chunks,)),
            dma((2,)), dma((per_home, 4)), dma(()), dma((2,)), dma((2,)), dma(()),
        ],
        compiler_params=pltpu.CompilerParams(
            collective_id=0, has_side_effects=True, vmem_limit_bytes=67043328),
        name='gla_layers',
    )(x, wq, wk, wv, wo, w1, w2, wa, beta, g1, go, g2)
    return outs[0], outs[1]


def solution(mesh, rows=256, tile=512, tile2=256):
    mat_spec = P('stage', None, None)
    vec_spec = P('stage', None)
    weight_specs = (vec_spec, mat_spec, mat_spec, mat_spec, mat_spec, vec_spec, vec_spec, mat_spec, vec_spec, mat_spec, mat_spec)

    def device_program(x_tokens, norm_attn, w_query, w_key, w_value, w_gate, gate_bias, norm_out, w_out, norm_mlp, w_up, w_down):
        heads = gate_bias.shape[1]
        val_dim = norm_out.shape[1]
        key_dim = w_query.shape[2] // heads
        wa = jnp.pad(w_gate[0], ((0, 0), (0, 128 - heads)))
        beta = jnp.pad(gate_bias, ((0, 0), (0, 128 - heads)))
        y, s = run_layers(
            rows, tile, tile2, x_tokens, w_query[0], w_key[0], w_value[0], w_out[0], w_up[0], w_down[0], wa, beta,
            norm_attn.astype(F32), norm_out.astype(F32), norm_mlp.astype(F32), heads)
        return y[None], s.reshape(1, x_tokens.shape[0], heads, key_dim, val_dim)

    return jax.shard_map(
        device_program,
        mesh=mesh,
        in_specs=(P('batch', 'seq', None),) + weight_specs,
        out_specs=(P('stage', 'batch', 'seq', None), P('stage', 'batch', None, None, None)),
        check_vma=False,
    )
```

time: 3450 us -> 717 us (0.21)
  waiting for transfers between devices: 2730 us -> 0 us
  Pallas kernels: 0 us -> 692 us
  matrix products: 506 us -> 0 us
  local copies, waits for them, and re-layouts: 113 us -> 19.6 us
  other arithmetic: 52 us -> 3.86 us
    ppermute x10 -> x0, waiting for transfers between devices: 2670 us -> none  [the longest x5 1620 us: step_body(): s_recv = lax.ppermute(s_done, 'seq', seq_pairs)]
    pallas_call x0 -> x1, Pallas kernels: none -> 692 us  [run_layers(): pl.pallas_call(functools.partial(layer_kernel, rows, heads, tile, tile2),...]
    dot_general x10 -> x0, matrix products: 506 us -> none  [the longest x1 145 us: finish_part(): jnp.einsum('bcf,fd->bcd', hidden, w_down, preferred_element_type=jnp.floa...]
    psum x1 -> x0, waiting for transfers between devices: 57.1 us -> none  [device_program(): s_final = lax.psum(jnp.where(seq_idx == num_shards - 1, s_done, 0.0), 'seq')]
    while x2 -> x0, local copies, waits for them, and re-layouts: 44.7 us -> none  [device_program(): lax.fori_loop(0, step_count, step_body, (zero_h, zero_s, zero_h, zero_s))]
  transfers between devices with their start and end apart: 11 -> 0, of which waited for: 11 -> 0; matrix products, arithmetic and copies ran while one was open for 1% -> 0% of each run, Pallas kernels for 0% -> 0%
where the time goes in v1:
time: 717 us; the launch traced here: 716 us
  Pallas kernels  692 us (97%)
  local copies, waits for them, and re-layouts  19.6 us (3%)
    pallas_call x1, Pallas kernels, run_layers(): pl.pallas_call(functools.partial(layer_kernel, rows, heads, tile, tile2),...  692 us
    unnamed x5, local copies, waits for them, and re-layouts  17.5 us

profile of v1, /device:TPU:7, one launch (start us, length us, event | category | flops | bytes accessed | tf_op | source)
XLA Modules:
  0.0 716.5 jit_solution(6953036662325505606)
XLA Ops:
  0.6 1.2 pad.9.beta
  1.9 1.3 convert_element_type.14.go
  3.1 1.3 convert_element_type.13.g1
  4.4 1.3 convert_element_type.15.g2
  5.7 1.0 copy.14
  6.8 0.9 pad.8.wa
  7.7 692.3 %gla_layers.1 = (bf16[2,2048,2048]{2,1,0:T(8,128)(2,1)}, f32[2,1024,512]{2,1,0:T(8,128)}, bf16[16,256,2048]{2,1,0:T(8,128)(2,1)}, bf16[16,256,2048]{2,1,0:T(8,128)(2,1)}) custom-call(bf16[2,2048,2048]{2,1,0:T(8,128)(2,1)} %x.5, bf16[2048,1024]{1,0:T(8,128)(2,1)} %bitcast.14, bf16[2048,1024]{1,0:T(8,128)(2,1)} %bitcast.15, bf16[2048,2048]{1,0:T(8,128)(2,1)} %bitcast.12, ...), custom_call_target="tpu_custom_call" | custom-call | tf_op jit(solution)/shard_map/gla_layers/pallas_call | solution.py:414
  700.0 0.0 copy-start
  700.0 14.5 %copy.17 = bf16[1,2,2048,2048]{3,2,1,0:T(8,128)(2,1)} copy(bf16[1,2,2048,2048]{3,2,1,0:T(8,128)(2,1)} %bitcast.11) | data formatting | bytes 33554432
  714.5 0.0 copy-done
  714.5 2.0 copy.18
Async XLA Ops:
  700.0 14.5 %copy-start = (f32[2,1024,512]{2,1,0:T(8,128)S(1)}, f32[2,1024,512]{2,1,0:T(8,128)}, u32[]{:S(2)}) copy-start(f32[2,1024,512]{2,1,0:T(8,128)} %get-tuple-element.5) | copy-start | bytes 12582916

commit v2 on v1

v2 whole, which is shorter than its diff:
```python
import functools

import jax
import jax.numpy as jnp
from jax import lax
from jax.experimental import pallas as pl
from jax.experimental.pallas import tpu as pltpu
from jax.sharding import PartitionSpec as P

NORM_EPS = 1e-6
MESH = pl.DeviceIdType.MESH
BF16 = jnp.bfloat16
F32 = jnp.float32
NUM_W = 5
NUM_W2 = 4
AHEAD = 2


def mean_sq_scale(values):
    return lax.rsqrt(jnp.mean(values * values, axis=-1, keepdims=True) + NORM_EPS)


def dot32(lhs, rhs):
    return jnp.dot(lhs, rhs, preferred_element_type=F32)


def layer_kernel(
    rows, heads, tile, tile2,
    x, wq, wk, wv, wo, w1, w2, wa, beta, g1, go, g2,
    y_out, s_out, xbuf, hbuf,
    wqkv, wbuf, w2buf, hin, u, r, hid, ybuf, state, s_in, l_own, l_recv, cum, cum_t, tril,
    wqkv_sem, w_sem, w2_sem, hin_sem, x_send, x_recv, h_send, h_recv, y_send, y_recv, l_send_sem, l_recv_sem, s_sem, s_recv_sem,
):
    stage = lax.axis_index('stage')
    me = lax.axis_index('seq')
    chip = lax.div(me, 2)
    core = lax.rem(me, 2)
    depth = x.shape[2]
    ffn = w1.shape[1]
    key_dim = wq.shape[1] // heads
    val_dim = wv.shape[1] // heads
    keys = heads * key_dim
    per_home = x.shape[1] // (2 * rows)
    chunks = 4 * per_home
    q_tiles = wq.shape[1] // tile
    v_tiles = wv.shape[1] // tile
    proj_tiles = 2 * q_tiles + v_tiles
    o_tiles = depth // tile
    up_tiles = w1.shape[1] // tile
    w_tiles = o_tiles + up_tiles
    down_tiles = depth // tile2
    last = chunks - 1

    def at(stage_pos, seq_pos):
        return {'stage': stage_pos, 'seq': seq_pos}

    def span(chunk, core_pos):
        return pl.ds(pl.multiple_of((lax.rem(chunk, per_home) * 2 + core_pos) * rows, rows), rows)

    def proj_copies():
        copies = []
        for i in range(q_tiles):
            copies.append(pltpu.make_async_copy(wk.at[:, pl.ds(i * tile, tile)], wqkv.at[i], wqkv_sem.at[i]))
        for i in range(v_tiles):
            n = q_tiles + i
            copies.append(pltpu.make_async_copy(wv.at[:, pl.ds(i * tile, tile)], wqkv.at[n], wqkv_sem.at[n]))
        for i in range(q_tiles):
            n = q_tiles + v_tiles + i
            copies.append(pltpu.make_async_copy(wq.at[:, pl.ds(i * tile, tile)], wqkv.at[n], wqkv_sem.at[n]))
        return copies

    def w_slot(chunk, i):
        if w_tiles % NUM_W == 0:
            return i % NUM_W
        return lax.rem(chunk * w_tiles + i, NUM_W)

    def start_w(i, slot):
        src = wo.at[:, pl.ds(i * tile, tile)] if i < o_tiles else w1.at[:, pl.ds((i - o_tiles) * tile, tile)]
        pltpu.make_async_copy(src, wbuf.at[slot], w_sem.at[slot]).start()

    def wait_w(chunk, i):
        slot = w_slot(chunk, i)
        pltpu.make_async_copy(w1.at[:, pl.ds(0, tile)], wbuf.at[slot], w_sem.at[slot]).wait()

    def next_w(chunk, i):
        slot = w_slot(chunk, i)
        if i + NUM_W < w_tiles:
            start_w(i + NUM_W, slot)
        else:
            @pl.when(chunk < last)
            def _():
                start_w(i + NUM_W - w_tiles, slot)

    def w2_copy(n, slot):
        return pltpu.make_async_copy(w2.at[:, pl.ds(n * tile2, tile2)], w2buf.at[slot], w2_sem.at[slot])

    def x_copy(chunk, dest):
        return pltpu.make_async_remote_copy(
            src_ref=x.at[dest // 2, span(chunk, dest % 2)],
            dst_ref=xbuf.at[chunk],
            send_sem=x_send.at[lax.rem(chunk, per_home), dest],
            recv_sem=x_recv.at[chunk],
            device_id=at(0, dest),
            device_id_type=MESH,
        )

    def x_mine(chunk, dest):
        home = lax.div(chunk, per_home)
        same = lax.div(home, 2) == dest // 2
        return (me == home) & (home != dest) & ((same & (stage == 0)) | ((lax.div(home, 2) != dest // 2) & (stage == dest % 2)))

    def push_x(chunk):
        for dest in range(4):
            @pl.when(x_mine(chunk, dest))
            def _():
                x_copy(chunk, dest).start()

    def landed(buf, sem, chunk):
        pltpu.make_async_remote_copy(
            src_ref=buf.at[chunk], dst_ref=buf.at[chunk], send_sem=x_send.at[0, 0], recv_sem=sem.at[chunk],
            device_id=at(stage, me), device_id_type=MESH,
        ).wait_recv()

    def load_h(chunk):
        slot = lax.rem(chunk, 2)
        local = me == lax.div(chunk, per_home)

        @pl.when((stage == 0) & local)
        def _():
            pltpu.make_async_copy(x.at[chip, span(chunk, core)], hin.at[slot], hin_sem.at[slot]).start()

        @pl.when((stage == 0) & (me != lax.div(chunk, per_home)))
        def _():
            landed(xbuf, x_recv, chunk)
            pltpu.make_async_copy(xbuf.at[chunk], hin.at[slot], hin_sem.at[slot]).start()

        @pl.when(stage == 1)
        def _():
            landed(hbuf, h_recv, chunk)
            pltpu.make_async_copy(hbuf.at[chunk], hin.at[slot], hin_sem.at[slot]).start()

    def part_cols(part):
        return slice(None) if part is None else pl.ds(part * 2 * tile2, 2 * tile2)

    def h_copy(chunk, part=None):
        slot = lax.rem(chunk, 2)
        return pltpu.make_async_remote_copy(
            src_ref=ybuf.at[slot, :, part_cols(part)], dst_ref=hbuf.at[chunk, :, part_cols(part)],
            send_sem=h_send.at[slot], recv_sem=h_recv.at[chunk],
            device_id=at(1, me), device_id_type=MESH,
        )

    def y_local(chunk, part=None):
        slot = lax.rem(chunk, 2)
        return pltpu.make_async_copy(
            ybuf.at[slot, :, part_cols(part)], y_out.at[chip, span(chunk, core), part_cols(part)], y_send.at[slot])

    def y_remote(chunk, part=None):
        slot = lax.rem(chunk, 2)
        return pltpu.make_async_remote_copy(
            src_ref=ybuf.at[slot, :, part_cols(part)], dst_ref=y_out.at[chip, span(chunk, core), part_cols(part)],
            send_sem=y_send.at[slot], recv_sem=y_recv.at[lax.rem(chunk, per_home), me],
            device_id=at(stage, lax.div(chunk, per_home)), device_id_type=MESH,
        )

    def send_y(chunk, part):
        @pl.when(stage == 0)
        def _():
            h_copy(chunk, part).start()

        @pl.when(me == lax.div(chunk, per_home))
        def _():
            y_local(chunk, part).start()

        @pl.when(me != lax.div(chunk, per_home))
        def _():
            y_remote(chunk, part).start()

    def sent_y(chunk):
        @pl.when(stage == 0)
        def _():
            h_copy(chunk).wait_send()

        @pl.when(me == lax.div(chunk, per_home))
        def _():
            y_local(chunk).wait()

        @pl.when(me != lax.div(chunk, per_home))
        def _():
            y_remote(chunk).wait_send()

    head_rows = key_dim + 8

    def l_copy(chunk, h):
        slot = lax.rem(chunk, 2)
        rng = pl.ds(h * head_rows, head_rows)
        return pltpu.make_async_remote_copy(
            src_ref=l_own.at[rng], dst_ref=l_recv.at[slot, rng],
            send_sem=l_send_sem.at[h], recv_sem=l_recv_sem.at[slot, h],
            device_id=at(stage, chip * 2 + 1 - core), device_id_type=MESH,
        )

    def s_rows(part):
        return pl.ds(pl.multiple_of(part * (keys // 2), keys // 2), keys // 2)

    def s_local():
        return pltpu.make_async_copy(state, s_out.at[chip], s_sem.at[0])

    def s_remote():
        return pltpu.make_async_remote_copy(
            src_ref=state.at[s_rows(core)], dst_ref=s_out.at[chip, s_rows(core)], send_sem=s_sem.at[1],
            recv_sem=s_recv_sem.at[core],
            device_id=at(stage, (1 - chip) * 2 + core), device_id_type=MESH,
        )

    def s_forward():
        part = s_out.at[1 - chip, s_rows(core)]
        return pltpu.make_async_remote_copy(
            src_ref=part, dst_ref=part, send_sem=s_sem.at[2], recv_sem=s_recv_sem.at[core],
            device_id=at(stage, chip * 2 + 1 - core), device_id_type=MESH,
        )

    def s_landed(part):
        ref = s_out.at[1 - chip, s_rows(part)]
        pltpu.make_async_remote_copy(
            src_ref=ref, dst_ref=ref, send_sem=s_sem.at[1], recv_sem=s_recv_sem.at[part],
            device_id=at(stage, me), device_id_type=MESH,
        ).wait_recv()

    barrier = pltpu.get_barrier_semaphore()
    for stage_pos in range(2):
        for seq_pos in range(4):
            pl.semaphore_signal(barrier, inc=1, device_id=at(stage_pos, seq_pos), device_id_type=MESH)
    pl.semaphore_wait(barrier, 8)

    for chunk in range(AHEAD):
        push_x(jnp.int32(chunk))
    first_copies = proj_copies()
    for copy in first_copies:
        copy.start()
    for i in range(NUM_W):
        start_w(i, i)
    for n in range(NUM_W2):
        w2_copy(n, n).start()
    state[...] = jnp.zeros_like(state)
    load_h(jnp.int32(0))
    for copy in first_copies:
        copy.wait()

    def project(n, dest, dest_col, scale):
        for part in range(2):
            half = tile // 2
            prod = dot32(u[...], wqkv[n, :, part * half:(part + 1) * half])
            if scale is not None:
                prod = prod * scale
            col = dest_col + part * half
            dest[:, col:col + half] = prod.astype(BF16)

    def norm_rows(read, gain, dest):
        step = min(16, rows)
        for i in range(rows // step):
            rng = slice(i * step, (i + 1) * step)
            vals = read(rng)
            dest[rng, :] = (vals * mean_sq_scale(vals) * gain[...]).astype(BF16)

    def q_of(h):
        return hid[:, h * key_dim:(h + 1) * key_dim]

    def k_of(h):
        return hid[:, keys + h * key_dim:keys + (h + 1) * key_dim]

    def v_of(h):
        return hid[:, 2 * keys + h * val_dim:2 * keys + (h + 1) * val_dim]

    def local_state(h):
        ci = cum[:, h:h + 1]
        total = cum[rows - 1:rows, h:h + 1]
        kd = (k_of(h).astype(F32) * jnp.exp(total - ci)).astype(BF16)
        base = h * head_rows
        l_own[base:base + key_dim, :] = lax.dot_general(
            kd, v_of(h), (((0,), (0,)), ((), ())), preferred_element_type=F32)
        l_own[base + key_dim:base + head_rows, :] = jnp.broadcast_to(jnp.exp(total), (8, val_dim))

    row_id = lax.broadcasted_iota(jnp.int32, (rows, rows), 0)
    col_id = lax.broadcasted_iota(jnp.int32, (rows, rows), 1)
    tril[...] = (row_id >= col_id).astype(F32).astype(BF16)

    def chunk_body(chunk, carry):
        slot = lax.rem(chunk, 2)

        @pl.when(chunk + AHEAD < chunks)
        def _():
            push_x(chunk + AHEAD)

        pltpu.make_async_copy(hbuf.at[0], hin.at[slot], hin_sem.at[slot]).wait()
        norm_rows(lambda rng: hin[slot, rng, :].astype(F32), g1, u)

        gate = dot32(u[...], wa[...]) + beta[...]
        log_decay = jnp.minimum(gate, 0.0) - jnp.log1p(jnp.exp(-jnp.abs(gate)))
        high = log_decay.astype(BF16)
        rest = log_decay - high.astype(F32)
        mid = rest.astype(BF16)
        low = (rest - mid.astype(F32)).astype(BF16)
        cum_val = dot32(tril[...], high) + (dot32(tril[...], mid) + dot32(tril[...], low))
        cum[...] = cum_val
        cum_t[...] = cum_val.T

        for h in range(heads):
            if h * key_dim % tile == 0:
                project(h * key_dim // tile, hid, keys + h * key_dim, key_dim ** -0.5)
            project(q_tiles + h, hid, 2 * keys + h * tile, None)
            local_state(h)
            l_copy(chunk, h).start()

        for i in range(q_tiles):
            project(q_tiles + v_tiles + i, hid, i * tile, None)
        for h in range(heads):
            ci = cum[:, h:h + 1]
            cj = cum_t[h:h + 1, :]
            scores = lax.dot_general(q_of(h), k_of(h), (((1,), (1,)), ((), ())), preferred_element_type=F32)
            decay = jnp.exp(jnp.where(row_id >= col_id, ci - cj, -jnp.inf))
            r[:, h * val_dim:(h + 1) * val_dim] = dot32((scores * decay).astype(BF16), v_of(h))

        first = core == 0

        def state_rows():
            step = min(32, key_dim)
            for h in range(heads):
                for i in range(key_dim // step):
                    sub = slice(h * key_dim + i * step, h * key_dim + (i + 1) * step)
                    lsub = slice(h * head_rows + i * step, h * head_rows + (i + 1) * step)
                    yield sub, lsub, slice(h * head_rows + key_dim, h * head_rows + key_dim + 1)

        @pl.when(core == 0)
        def _():
            for sub, lsub, row in state_rows():
                s_in[sub, :] = state[sub, :].astype(BF16)

        @pl.when(core == 1)
        def _():
            for h in range(heads):
                l_copy(chunk, h).wait_recv()
            for sub, lsub, row in state_rows():
                s_in[sub, :] = (state[sub, :] * l_recv[slot, row, :] + l_recv[slot, lsub, :]).astype(BF16)

        wait_w(chunk, 0)
        wait_w(chunk, 1)
        for h in range(heads):
            col = slice(h * val_dim, (h + 1) * val_dim)
            inter = dot32(q_of(h), s_in[h * key_dim:(h + 1) * key_dim, :])
            o_val = r[:, col] + inter * jnp.exp(cum[:, h:h + 1])
            u[:, col] = (o_val * mean_sq_scale(o_val) * go[...]).astype(BF16)

        def next_state():
            for sub, lsub, row in state_rows():
                ours = l_own[lsub, :]
                theirs = l_recv[slot, lsub, :]
                d_own = l_own[row, :]
                d_other = l_recv[slot, row, :]
                mid = state[sub, :] * jnp.where(first, d_own, d_other) + jnp.where(first, ours, theirs)
                state[sub, :] = mid * jnp.where(first, d_other, d_own) + jnp.where(first, theirs, ours)

        def out_proj(i):
            wslot = w_slot(chunk, i)
            for part in range(2):
                half = tile // 2
                col = slice(i * tile + part * half, i * tile + (part + 1) * half)
                r[:, col] = hin[slot, :, col].astype(F32) + dot32(u[...], wbuf[wslot, :, part * half:(part + 1) * half])

        for pair in range(0, o_tiles, 2):
            group = range(pair, min(pair + 2, o_tiles))
            if pair:
                for i in group:
                    wait_w(chunk, i)
            if pair + 2 >= o_tiles:
                @pl.when(core == 0)
                def _():
                    for h in range(heads):
                        l_copy(chunk, h).wait_recv()

                for h in range(heads):
                    l_copy(chunk, h).wait_send()
                next_state()
            for i in group:
                out_proj(i)
            for i in group:
                next_w(chunk, i)

        @pl.when(chunk == last)
        def _():
            s_local().start()
            s_remote().start()

        norm_rows(lambda rng: r[rng, :], g2, u)

        for pair in range(o_tiles, w_tiles, 2):
            group = range(pair, min(pair + 2, w_tiles))
            for i in group:
                wait_w(chunk, i)
            for i in group:
                wslot = w_slot(chunk, i)
                for part in range(2):
                    half = tile // 2
                    col = (i - o_tiles) * tile + part * half
                    prod = dot32(u[...], wbuf[wslot, :, part * half:(part + 1) * half])
                    hid[:, col:col + half] = jax.nn.gelu(prod, approximate=True).astype(BF16)
            for i in group:
                next_w(chunk, i)

        @pl.when(chunk >= 2)
        def _():
            sent_y(chunk - 2)

        for n in range(down_tiles):
            w2_copy(n, n % NUM_W2).wait()
            if n == down_tiles - 2:
                @pl.when(chunk < last)
                def _():
                    load_h(chunk + 1)
            col = slice(n * tile2, (n + 1) * tile2)
            ybuf[slot, :, col] = (r[:, col] + dot32(hid[:, :ffn], w2buf[n % NUM_W2])).astype(BF16)
            following = n + NUM_W2
            if following < down_tiles:
                w2_copy(following, n % NUM_W2).start()
            else:
                @pl.when(chunk < last)
                def _():
                    w2_copy(following - down_tiles, n % NUM_W2).start()
            if n % 2 == 1:
                send_y(chunk, n // 2)
        return carry

    lax.fori_loop(0, chunks, chunk_body, 0)

    s_local().wait()
    s_remote().wait_send()
    s_landed(core)
    s_forward().start()
    s_forward().wait_send()
    s_landed(1 - core)
    sent_y(jnp.int32(chunks - 2))
    sent_y(jnp.int32(chunks - 1))

    def x_done(chunk, carry):
        for dest in range(4):
            @pl.when(x_mine(chunk, dest))
            def _():
                x_copy(chunk, dest).wait_send()
        return carry

    lax.fori_loop(0, chunks, x_done, 0)

    def y_done(e, carry):
        for src in range(4):
            @pl.when(me != src)
            def _():
                pltpu.make_async_remote_copy(
                    src_ref=ybuf.at[0], dst_ref=y_out.at[src // 2, span(e, src % 2)], send_sem=y_send.at[0],
                    recv_sem=y_recv.at[e, src], device_id=at(stage, me), device_id_type=MESH,
                ).wait_recv()
        return carry

    lax.fori_loop(0, per_home, y_done, 0)


def run_layers(rows, tile, tile2, x, wq, wk, wv, wo, w1, w2, wa, beta, g1, go, g2, heads):
    seqs, tok_len, depth = x.shape
    keys, values, ffn = wq.shape[1], wv.shape[1], w1.shape[1]
    key_dim, val_dim = keys // heads, values // heads
    per_home = tok_len // (2 * rows)
    chunks = 4 * per_home
    proj_tiles = (2 * keys + values) // tile
    hbm = pl.BlockSpec(memory_space=pl.ANY)
    vmem = pl.BlockSpec(memory_space=pltpu.VMEM)
    dma = pltpu.SemaphoreType.DMA
    outs = pl.pallas_call(
        functools.partial(layer_kernel, rows, heads, tile, tile2),
        out_shape=(
            jax.ShapeDtypeStruct((seqs, tok_len, depth), BF16),
            jax.ShapeDtypeStruct((seqs, keys, val_dim), F32),
            jax.ShapeDtypeStruct((chunks, rows, depth), BF16),
            jax.ShapeDtypeStruct((chunks, rows, depth), BF16),
        ),
        in_specs=[hbm] * 7 + [vmem] * 5,
        out_specs=(hbm, hbm, hbm, hbm),
        scratch_shapes=[
            pltpu.VMEM((proj_tiles, depth, tile), BF16),
            pltpu.VMEM((NUM_W, depth, tile), BF16),
            pltpu.VMEM((NUM_W2, ffn, tile2), BF16),
            pltpu.VMEM((2, rows, depth), BF16),
            pltpu.VMEM((rows, depth), BF16),
            pltpu.VMEM((rows, depth), F32),
            pltpu.VMEM((rows, max(ffn, 2 * keys + values)), BF16),
            pltpu.VMEM((2, rows, depth), BF16),
            pltpu.VMEM((keys, val_dim), F32),
            pltpu.VMEM((keys, val_dim), BF16),
            pltpu.VMEM((keys + 8 * heads, val_dim), F32),
            pltpu.VMEM((2, keys + 8 * heads, val_dim), F32),
            pltpu.VMEM((rows, 128), F32),
            pltpu.VMEM((128, rows), F32),
            pltpu.VMEM((rows, rows), BF16),
            dma((proj_tiles,)), dma((NUM_W,)), dma((NUM_W2,)), dma((2,)),
            dma((per_home, 4)), dma((chunks,)), dma((2,)), dma((chunks,)),
            dma((2,)), dma((per_home, 4)), dma((heads,)), dma((2, heads)), dma((3,)), dma((2,)),
        ],
        compiler_params=pltpu.CompilerParams(
            collective_id=0, has_side_effects=True, vmem_limit_bytes=67043328),
        name='gla_layers',
    )(x, wq, wk, wv, wo, w1, w2, wa, beta, g1, go, g2)
    return outs[0], outs[1]


def solution(mesh, rows=256, tile=512, tile2=256):
    mat_spec = P('stage', None, None)
    vec_spec = P('stage', None)
    weight_specs = (vec_spec, mat_spec, mat_spec, mat_spec, mat_spec, vec_spec, vec_spec, mat_spec, vec_spec, mat_spec, mat_spec)

    def device_program(x_tokens, norm_attn, w_query, w_key, w_value, w_gate, gate_bias, norm_out, w_out, norm_mlp, w_up, w_down):
        heads = gate_bias.shape[1]
        val_dim = norm_out.shape[1]
        key_dim = w_query.shape[2] // heads
        wa = jnp.pad(w_gate[0], ((0, 0), (0, 128 - heads)))
        beta = jnp.pad(gate_bias, ((0, 0), (0, 128 - heads)))
        y, s = run_layers(
            rows, tile, tile2, x_tokens, w_query[0], w_key[0], w_value[0], w_out[0], w_up[0], w_down[0], wa, beta,
            norm_attn.astype(F32), norm_out.astype(F32), norm_mlp.astype(F32), heads)
        return y[None], s.reshape(1, x_tokens.shape[0], heads, key_dim, val_dim)

    return jax.shard_map(
        device_program,
        mesh=mesh,
        in_specs=(P('batch', 'seq', None),) + weight_specs,
        out_specs=(P('stage', 'batch', 'seq', None), P('stage', 'batch', None, None, None)),
        check_vma=False,
    )
```

time: 717 us -> 664 us (0.926)
  Pallas kernels: 692 us -> 639 us
    pallas_call x1, Pallas kernels: 692 us -> 639 us  [run_layers(): pl.pallas_call(functools.partial(layer_kernel, rows, heads, tile, tile2),...]
where the time goes in v2:
time: 664 us; the launch traced here: 663 us
  Pallas kernels  639 us (96%)
  local copies, waits for them, and re-layouts  19.6 us (3%)
    pallas_call x1, Pallas kernels, run_layers(): pl.pallas_call(functools.partial(layer_kernel, rows, heads, tile, tile2),...  639 us
    unnamed x5, local copies, waits for them, and re-layouts  17.5 us

profile of v2, /device:TPU:7, one launch (start us, length us, event | category | flops | bytes accessed | tf_op | source)
XLA Modules:
  0.0 663.3 jit_solution(1513228680058809516)
XLA Ops:
  0.6 1.2 pad.9.beta
  1.9 1.3 convert_element_type.14.go
  3.1 1.3 convert_element_type.13.g1
  4.4 1.3 convert_element_type.15.g2
  5.7 1.0 copy.14
  6.8 0.9 pad.8.wa
  7.7 639.1 %gla_layers.1 = (bf16[2,2048,2048]{2,1,0:T(8,128)(2,1)}, f32[2,1024,512]{2,1,0:T(8,128)}, bf16[16,256,2048]{2,1,0:T(8,128)(2,1)}, bf16[16,256,2048]{2,1,0:T(8,128)(2,1)}) custom-call(bf16[2,2048,2048]{2,1,0:T(8,128)(2,1)} %x.5, bf16[2048,1024]{1,0:T(8,128)(2,1)} %bitcast.14, bf16[2048,1024]{1,0:T(8,128)(2,1)} %bitcast.15, bf16[2048,2048]{1,0:T(8,128)(2,1)} %bitcast.12, ...), custom_call_target="tpu_custom_call" | custom-call | tf_op jit(solution)/shard_map/gla_layers/pallas_call | solution.py:476
  646.8 0.0 copy-start
  646.8 14.5 %copy.17 = bf16[1,2,2048,2048]{3,2,1,0:T(8,128)(2,1)} copy(bf16[1,2,2048,2048]{3,2,1,0:T(8,128)(2,1)} %bitcast.11) | data formatting | bytes 33554432
  661.3 0.0 copy-done
  661.3 2.0 copy.18
Async XLA Ops:
  646.8 14.5 %copy-start = (f32[2,1024,512]{2,1,0:T(8,128)S(1)}, f32[2,1024,512]{2,1,0:T(8,128)}, u32[]{:S(2)}) copy-start(f32[2,1024,512]{2,1,0:T(8,128)} %get-tuple-element.5) | copy-start | bytes 12582916

commit v3 on v2

--- a/solution.py
+++ b/solution.py
@@ -12,7 +12,7 @@
 BF16 = jnp.bfloat16
 F32 = jnp.float32
 NUM_W = 5
-NUM_W2 = 4
+NUM_W2 = 2
 AHEAD = 2
 
 
@@ -28,7 +28,7 @@
     rows, heads, tile, tile2,
     x, wq, wk, wv, wo, w1, w2, wa, beta, g1, go, g2,
     y_out, s_out, xbuf, hbuf,
-    wqkv, wbuf, w2buf, hin, u, r, hid, ybuf, state, s_in, l_own, l_recv, cum, cum_t, tril,
+    wqkv, wbuf, w2buf, hin, u, r, hid, ybuf, state, s_in, l_own, l_recv, cum, cum_t, tril, raw,
     wqkv_sem, w_sem, w2_sem, hin_sem, x_send, x_recv, h_send, h_recv, y_send, y_recv, l_send_sem, l_recv_sem, s_sem, s_recv_sem,
 ):
     stage = lax.axis_index('stage')
@@ -91,8 +91,12 @@
             def _():
                 start_w(i + NUM_W - w_tiles, slot)
 
-    def w2_copy(n, slot):
-        return pltpu.make_async_copy(w2.at[:, pl.ds(n * tile2, tile2)], w2buf.at[slot], w2_sem.at[slot])
+    ffn_half = ffn // 2
+
+    def w2_copy(n, part):
+        slot = (n % NUM_W2) * 2 + part
+        src = w2.at[pl.ds(part * ffn_half, ffn_half), pl.ds(n * tile2, tile2)]
+        return pltpu.make_async_copy(src, w2buf.at[slot], w2_sem.at[slot])
 
     def x_copy(chunk, dest):
         return pltpu.make_async_remote_copy(
@@ -140,7 +144,7 @@
             pltpu.make_async_copy(hbuf.at[chunk], hin.at[slot], hin_sem.at[slot]).start()
 
     def part_cols(part):
-        return slice(None) if part is None else pl.ds(part * 2 * tile2, 2 * tile2)
+        return slice(None) if part is None else pl.ds(part * tile2, tile2)
 
     def h_copy(chunk, part=None):
         slot = lax.rem(chunk, 2)
@@ -241,7 +245,8 @@
     for i in range(NUM_W):
         start_w(i, i)
     for n in range(NUM_W2):
-        w2_copy(n, n).start()
+        for part in range(2):
+            w2_copy(n, part).start()
     state[...] = jnp.zeros_like(state)
     load_h(jnp.int32(0))
     for copy in first_copies:
@@ -305,15 +310,20 @@
         cum[...] = cum_val
         cum_t[...] = cum_val.T
 
+        project(0, hid, keys, key_dim ** -0.5)
+        project(q_tiles, hid, 2 * keys, None)
         for h in range(heads):
-            if h * key_dim % tile == 0:
-                project(h * key_dim // tile, hid, keys + h * key_dim, key_dim ** -0.5)
-            project(q_tiles + h, hid, 2 * keys + h * tile, None)
+            if h + 1 < heads:
+                if (h + 1) * key_dim % tile == 0:
+                    n = (h + 1) * key_dim // tile
+                    project(n, hid, keys + n * tile, key_dim ** -0.5)
+                project(q_tiles + h + 1, hid, 2 * keys + (h + 1) * tile, None)
+            else:
+                for i in range(q_tiles):
+                    project(q_tiles + v_tiles + i, hid, i * tile, None)
             local_state(h)
             l_copy(chunk, h).start()
 
-        for i in range(q_tiles):
-            project(q_tiles + v_tiles + i, hid, i * tile, None)
         for h in range(heads):
             ci = cum[:, h:h + 1]
             cj = cum_t[h:h + 1, :]
@@ -323,9 +333,9 @@
 
         first = core == 0
 
-        def state_rows():
+        def state_rows(these=range(heads)):
             step = min(32, key_dim)
-            for h in range(heads):
+            for h in these:
                 for i in range(key_dim // step):
                     sub = slice(h * key_dim + i * step, h * key_dim + (i + 1) * step)
                     lsub = slice(h * head_rows + i * step, h * head_rows + (i + 1) * step)
@@ -351,8 +361,8 @@
             o_val = r[:, col] + inter * jnp.exp(cum[:, h:h + 1])
             u[:, col] = (o_val * mean_sq_scale(o_val) * go[...]).astype(BF16)
 
-        def next_state():
-            for sub, lsub, row in state_rows():
+        def next_state(h):
+            for sub, lsub, row in state_rows((h,)):
                 ours = l_own[lsub, :]
                 theirs = l_recv[slot, lsub, :]
                 d_own = l_own[row, :]
@@ -372,62 +382,79 @@
             if pair:
                 for i in group:
                     wait_w(chunk, i)
-            if pair + 2 >= o_tiles:
-                @pl.when(core == 0)
-                def _():
-                    for h in range(heads):
-                        l_copy(chunk, h).wait_recv()
-
-                for h in range(heads):
-                    l_copy(chunk, h).wait_send()
-                next_state()
             for i in group:
                 out_proj(i)
             for i in group:
                 next_w(chunk, i)
 
-        @pl.when(chunk == last)
-        def _():
-            s_local().start()
-            s_remote().start()
-
+        @pl.when(core == 0)
+        def _():
+            for h in range(heads):
+                l_copy(chunk, h).wait_recv()
+
+        for h in range(heads):
+            l_copy(chunk, h).wait_send()
         norm_rows(lambda rng: r[rng, :], g2, u)
 
+        half = tile // 2
+        staged = None
         for pair in range(o_tiles, w_tiles, 2):
             group = range(pair, min(pair + 2, w_tiles))
             for i in group:
                 wait_w(chunk, i)
+            if staged is not None:
+                hid[:, staged:staged + half] = jax.nn.gelu(raw[...], approximate=True).astype(BF16)
             for i in group:
                 wslot = w_slot(chunk, i)
                 for part in range(2):
-                    half = tile // 2
                     col = (i - o_tiles) * tile + part * half
                     prod = dot32(u[...], wbuf[wslot, :, part * half:(part + 1) * half])
-                    hid[:, col:col + half] = jax.nn.gelu(prod, approximate=True).astype(BF16)
+                    if i == group[-1] and part == 1 and i + 1 < w_tiles:
+                        raw[...] = prod
+                        staged = col
+                    else:
+                        hid[:, col:col + half] = jax.nn.gelu(prod, approximate=True).astype(BF16)
+            h = (pair - o_tiles) // 2
+            if h < heads:
+                next_state(h)
             for i in group:
                 next_w(chunk, i)
 
+        @pl.when(chunk == last)
+        def _():
+            s_local().start()
+            s_remote().start()
+
         @pl.when(chunk >= 2)
         def _():
             sent_y(chunk - 2)
 
         for n in range(down_tiles):
-            w2_copy(n, n % NUM_W2).wait()
-            if n == down_tiles - 2:
+            for part in range(2):
+                w2_copy(n, part).wait()
+            if n == down_tiles - 1:
                 @pl.when(chunk < last)
                 def _():
                     load_h(chunk + 1)
             col = slice(n * tile2, (n + 1) * tile2)
-            ybuf[slot, :, col] = (r[:, col] + dot32(hid[:, :ffn], w2buf[n % NUM_W2])).astype(BF16)
+            wslot = (n % NUM_W2) * 2
+            front = dot32(hid[:, :ffn_half], w2buf[wslot])
             following = n + NUM_W2
             if following < down_tiles:
-                w2_copy(following, n % NUM_W2).start()
+                w2_copy(following, 0).start()
             else:
                 @pl.when(chunk < last)
                 def _():
-                    w2_copy(following - down_tiles, n % NUM_W2).start()
-            if n % 2 == 1:
-                send_y(chunk, n // 2)
+                    w2_copy(following - down_tiles, 0).start()
+            back = dot32(hid[:, ffn_half:ffn], w2buf[wslot + 1])
+            ybuf[slot, :, col] = (r[:, col] + (front + back)).astype(BF16)
+            if following < down_tiles:
+                w2_copy(following, 1).start()
+            else:
+                @pl.when(chunk < last)
+                def _():
+                    w2_copy(following - down_tiles, 1).start()
+            send_y(chunk, n)
         return carry
 
     lax.fori_loop(0, chunks, chunk_body, 0)
@@ -486,7 +513,7 @@
         scratch_shapes=[
             pltpu.VMEM((proj_tiles, depth, tile), BF16),
             pltpu.VMEM((NUM_W, depth, tile), BF16),
-            pltpu.VMEM((NUM_W2, ffn, tile2), BF16),
+            pltpu.VMEM((2 * NUM_W2, ffn // 2, tile2), BF16),
             pltpu.VMEM((2, rows, depth), BF16),
             pltpu.VMEM((rows, depth), BF16),
             pltpu.VMEM((rows, depth), F32),
@@ -499,7 +526,8 @@
             pltpu.VMEM((rows, 128), F32),
             pltpu.VMEM((128, rows), F32),
             pltpu.VMEM((rows, rows), BF16),
-            dma((proj_tiles,)), dma((NUM_W,)), dma((NUM_W2,)), dma((2,)),
+            pltpu.VMEM((rows, tile // 2), F32),
+            dma((proj_tiles,)), dma((NUM_W,)), dma((2 * NUM_W2,)), dma((2,)),
             dma((per_home, 4)), dma((chunks,)), dma((2,)), dma((chunks,)),
             dma((2,)), dma((per_home, 4)), dma((heads,)), dma((2, heads)), dma((3,)), dma((2,)),
         ],
@@ -510,7 +538,7 @@
     return outs[0], outs[1]
 
 
-def solution(mesh, rows=256, tile=512, tile2=256):
+def solution(mesh, rows=256, tile=512, tile2=512):
     mat_spec = P('stage', None, None)
     vec_spec = P('stage', None)
     weight_specs = (vec_spec, mat_spec, mat_spec, mat_spec, mat_spec, vec_spec, vec_spec, mat_spec, vec_spec, mat_spec, mat_spec)

time: 664 us -> 603 us (0.908)
  Pallas kernels: 639 us -> 578 us
    pallas_call x1, Pallas kernels: 639 us -> 578 us  [run_layers(): pl.pallas_call(functools.partial(layer_kernel, rows, heads, tile, tile2),...]
where the time goes in v3:
time: 603 us
  Pallas kernels  578 us (96%)
  local copies, waits for them, and re-layouts  19.6 us (3%)
    pallas_call x1, Pallas kernels, run_layers(): pl.pallas_call(functools.partial(layer_kernel, rows, heads, tile, tile2),...  578 us
    unnamed x5, local copies, waits for them, and re-layouts  17.5 us

profile of v3, /device:TPU:7, one launch (start us, length us, event | category | flops | bytes accessed | tf_op | source)
XLA Modules:
  0.0 602.6 jit_solution(7101522913225268222)
XLA Ops:
  0.6 1.2 pad.9.beta
  1.9 1.3 convert_element_type.14.go
  3.1 1.3 convert_element_type.13.g1
  4.4 1.3 convert_element_type.15.g2
  5.7 1.0 copy.14
  6.8 0.9 pad.8.wa
  7.7 578.5 %gla_layers.1 = (bf16[2,2048,2048]{2,1,0:T(8,128)(2,1)}, f32[2,1024,512]{2,1,0:T(8,128)}, bf16[16,256,2048]{2,1,0:T(8,128)(2,1)}, bf16[16,256,2048]{2,1,0:T(8,128)(2,1)}) custom-call(bf16[2,2048,2048]{2,1,0:T(8,128)(2,1)} %x.5, bf16[2048,1024]{1,0:T(8,128)(2,1)} %bitcast.14, bf16[2048,1024]{1,0:T(8,128)(2,1)} %bitcast.15, bf16[2048,2048]{1,0:T(8,128)(2,1)} %bitcast.12, ...), custom_call_target="tpu_custom_call" | custom-call | tf_op jit(solution)/shard_map/gla_layers/pallas_call | solution.py:503
  586.2 0.0 copy-start
  586.2 14.5 %copy.17 = bf16[1,2,2048,2048]{3,2,1,0:T(8,128)(2,1)} copy(bf16[1,2,2048,2048]{3,2,1,0:T(8,128)(2,1)} %bitcast.11) | data formatting | bytes 33554432
  600.6 0.0 copy-done
  600.6 2.0 copy.18
Async XLA Ops:
  586.2 14.5 %copy-start = (f32[2,1024,512]{2,1,0:T(8,128)S(1)}, f32[2,1024,512]{2,1,0:T(8,128)}, u32[]{:S(2)}) copy-start(f32[2,1024,512]{2,1,0:T(8,128)} %get-tuple-element.5) | copy-start | bytes 12582916

commit v4 on v3

--- a/solution.py
+++ b/solution.py
@@ -26,9 +26,9 @@
 
 def layer_kernel(
     rows, heads, tile, tile2,
-    x, wq, wk, wv, wo, w1, w2, wa, beta, g1, go, g2,
+    x, wq, wk, wv, wo, w1, w2, wa_in, beta_in, g1_in, go_in, g2_in,
     y_out, s_out, xbuf, hbuf,
-    wqkv, wbuf, w2buf, hin, u, r, hid, ybuf, state, s_in, l_own, l_recv, cum, cum_t, tril, raw,
+    wqkv, wbuf, w2buf, hin, u, r, hid, ybuf, state, s_in, l_own, l_recv, cum, cum_t, tril, raw, wa, beta, g1, go, g2,
     wqkv_sem, w_sem, w2_sem, hin_sem, x_send, x_recv, h_send, h_recv, y_send, y_recv, l_send_sem, l_recv_sem, s_sem, s_recv_sem,
 ):
     stage = lax.axis_index('stage')
@@ -195,12 +195,12 @@
 
     head_rows = key_dim + 8
 
-    def l_copy(chunk, h):
+    def l_copy(chunk, part):
         slot = lax.rem(chunk, 2)
-        rng = pl.ds(h * head_rows, head_rows)
+        rng = pl.ds(part * (heads // 2) * head_rows, (heads // 2) * head_rows)
         return pltpu.make_async_remote_copy(
             src_ref=l_own.at[rng], dst_ref=l_recv.at[slot, rng],
-            send_sem=l_send_sem.at[h], recv_sem=l_recv_sem.at[slot, h],
+            send_sem=l_send_sem.at[part], recv_sem=l_recv_sem.at[slot, part],
             device_id=at(stage, chip * 2 + 1 - core), device_id_type=MESH,
         )
 
@@ -247,8 +247,18 @@
     for n in range(NUM_W2):
         for part in range(2):
             w2_copy(n, part).start()
+    load_h(jnp.int32(0))
     state[...] = jnp.zeros_like(state)
-    load_h(jnp.int32(0))
+    g1[...] = g1_in[...].astype(F32)
+    go[...] = go_in[...].astype(F32)
+    g2[...] = g2_in[...].astype(F32)
+    beta[...] = jnp.zeros_like(beta)
+    beta[:, :heads] = beta_in[...]
+    lanes = wa.shape[1]
+    l_own[:lanes, :] = jnp.zeros((lanes, val_dim), F32)
+    for i in range(depth // val_dim):
+        l_own[:heads, :] = wa_in[:, i * val_dim:(i + 1) * val_dim].astype(F32)
+        wa[i * val_dim:(i + 1) * val_dim, :] = l_own[:lanes, :].T.astype(BF16)
     for copy in first_copies:
         copy.wait()
 
@@ -310,26 +320,20 @@
         cum[...] = cum_val
         cum_t[...] = cum_val.T
 
-        project(0, hid, keys, key_dim ** -0.5)
-        project(q_tiles, hid, 2 * keys, None)
-        for h in range(heads):
-            if h + 1 < heads:
-                if (h + 1) * key_dim % tile == 0:
-                    n = (h + 1) * key_dim // tile
-                    project(n, hid, keys + n * tile, key_dim ** -0.5)
-                project(q_tiles + h + 1, hid, 2 * keys + (h + 1) * tile, None)
-            else:
-                for i in range(q_tiles):
-                    project(q_tiles + v_tiles + i, hid, i * tile, None)
+        heads_half = heads // 2
+        for i in range(q_tiles):
+            project(i, hid, keys + i * tile, key_dim ** -0.5)
+        for i in range(v_tiles - 1):
+            project(q_tiles + i, hid, 2 * keys + i * tile, None)
+        for h in range(heads_half):
             local_state(h)
-            l_copy(chunk, h).start()
-
-        for h in range(heads):
-            ci = cum[:, h:h + 1]
-            cj = cum_t[h:h + 1, :]
-            scores = lax.dot_general(q_of(h), k_of(h), (((1,), (1,)), ((), ())), preferred_element_type=F32)
-            decay = jnp.exp(jnp.where(row_id >= col_id, ci - cj, -jnp.inf))
-            r[:, h * val_dim:(h + 1) * val_dim] = dot32((scores * decay).astype(BF16), v_of(h))
+        l_copy(chunk, 0).start()
+        project(q_tiles + v_tiles - 1, hid, 2 * keys + (v_tiles - 1) * tile, None)
+        for i in range(q_tiles):
+            project(q_tiles + v_tiles + i, hid, i * tile, None)
+        for h in range(heads_half, heads):
+            local_state(h)
+        l_copy(chunk, 1).start()
 
         first = core == 0
 
@@ -348,13 +352,20 @@
 
         @pl.when(core == 1)
         def _():
-            for h in range(heads):
-                l_copy(chunk, h).wait_recv()
+            for part in range(2):
+                l_copy(chunk, part).wait_recv()
             for sub, lsub, row in state_rows():
                 s_in[sub, :] = (state[sub, :] * l_recv[slot, row, :] + l_recv[slot, lsub, :]).astype(BF16)
 
         wait_w(chunk, 0)
         wait_w(chunk, 1)
+        for h in range(heads):
+            ci = cum[:, h:h + 1]
+            cj = cum_t[h:h + 1, :]
+            scores = lax.dot_general(q_of(h), k_of(h), (((1,), (1,)), ((), ())), preferred_element_type=F32)
+            decay = jnp.exp(jnp.where(row_id >= col_id, ci - cj, -jnp.inf))
+            r[:, h * val_dim:(h + 1) * val_dim] = dot32((scores * decay).astype(BF16), v_of(h))
+
         for h in range(heads):
             col = slice(h * val_dim, (h + 1) * val_dim)
             inter = dot32(q_of(h), s_in[h * key_dim:(h + 1) * key_dim, :])
@@ -387,19 +398,21 @@
             for i in group:
                 next_w(chunk, i)
 
-        @pl.when(core == 0)
-        def _():
-            for h in range(heads):
-                l_copy(chunk, h).wait_recv()
-
-        for h in range(heads):
-            l_copy(chunk, h).wait_send()
         norm_rows(lambda rng: r[rng, :], g2, u)
 
         half = tile // 2
         staged = None
         for pair in range(o_tiles, w_tiles, 2):
             group = range(pair, min(pair + 2, w_tiles))
+            h = (pair - o_tiles) // 2 - 1
+            if h == 0:
+                @pl.when(core == 0)
+                def _():
+                    for part in range(2):
+                        l_copy(chunk, part).wait_recv()
+
+                for part in range(2):
+                    l_copy(chunk, part).wait_send()
             for i in group:
                 wait_w(chunk, i)
             if staged is not None:
@@ -414,8 +427,7 @@
                         staged = col
                     else:
                         hid[:, col:col + half] = jax.nn.gelu(prod, approximate=True).astype(BF16)
-            h = (pair - o_tiles) // 2
-            if h < heads:
+            if 0 <= h < heads:
                 next_state(h)
             for i in group:
                 next_w(chunk, i)
@@ -527,9 +539,14 @@
             pltpu.VMEM((128, rows), F32),
             pltpu.VMEM((rows, rows), BF16),
             pltpu.VMEM((rows, tile // 2), F32),
+            pltpu.VMEM((depth, 128), BF16),
+            pltpu.VMEM((1, 128), F32),
+            pltpu.VMEM((1, depth), F32),
+            pltpu.VMEM((1, val_dim), F32),
+            pltpu.VMEM((1, depth), F32),
             dma((proj_tiles,)), dma((NUM_W,)), dma((2 * NUM_W2,)), dma((2,)),
             dma((per_home, 4)), dma((chunks,)), dma((2,)), dma((chunks,)),
-            dma((2,)), dma((per_home, 4)), dma((heads,)), dma((2, heads)), dma((3,)), dma((2,)),
+            dma((2,)), dma((per_home, 4)), dma((2,)), dma((2, 2)), dma((3,)), dma((2,)),
         ],
         compiler_params=pltpu.CompilerParams(
             collective_id=0, has_side_effects=True, vmem_limit_bytes=67043328),
@@ -547,11 +564,9 @@
         heads = gate_bias.shape[1]
         val_dim = norm_out.shape[1]
         key_dim = w_query.shape[2] // heads
-        wa = jnp.pad(w_gate[0], ((0, 0), (0, 128 - heads)))
-        beta = jnp.pad(gate_bias, ((0, 0), (0, 128 - heads)))
         y, s = run_layers(
-            rows, tile, tile2, x_tokens, w_query[0], w_key[0], w_value[0], w_out[0], w_up[0], w_down[0], wa, beta,
-            norm_attn.astype(F32), norm_out.astype(F32), norm_mlp.astype(F32), heads)
+            rows, tile, tile2, x_tokens, w_query[0], w_key[0], w_value[0], w_out[0], w_up[0], w_down[0], w_gate[0].T, gate_bias,
+            norm_attn, norm_out, norm_mlp, heads)
         return y[None], s.reshape(1, x_tokens.shape[0], heads, key_dim, val_dim)
 
     return jax.shard_map(

time: 603 us -> 580 us (0.962)
  Pallas kernels: 578 us -> 563 us
    pallas_call x1, Pallas kernels: 578 us -> 563 us  [run_layers(): pl.pallas_call(functools.partial(layer_kernel, rows, heads, tile, tile2),...]
    unnamed x5 -> x4, local copies, waits for them, and re-layouts: 17.5 us -> 16.5 us
where the time goes in v4:
time: 580 us
  Pallas kernels  563 us (97%)
  local copies, waits for them, and re-layouts  16.5 us (3%)
    pallas_call x1, Pallas kernels, run_layers(): pl.pallas_call(functools.partial(layer_kernel, rows, heads, tile, tile2),...  563 us
    unnamed x4, local copies, waits for them, and re-layouts  16.5 us

profile of v4, /device:TPU:7, one launch (start us, length us, event | category | flops | bytes accessed | tf_op | source)
XLA Modules:
  0.0 580.0 jit_solution(561026188491251246)
XLA Ops:
  0.6 562.9 %gla_layers.1 = (bf16[2,2048,2048]{2,1,0:T(8,128)(2,1)}, f32[2,1024,512]{2,1,0:T(8,128)}, bf16[16,256,2048]{2,1,0:T(8,128)(2,1)}, bf16[16,256,2048]{2,1,0:T(8,128)(2,1)}) custom-call(bf16[2,2048,2048]{2,1,0:T(8,128)(2,1)} %x.1, bf16[2048,1024]{1,0:T(8,128)(2,1)} %bitcast.17, bf16[2048,1024]{1,0:T(8,128)(2,1)} %bitcast.18, bf16[2048,2048]{1,0:T(8,128)(2,1)} %bitcast.14, ...), custom_call_target="tpu_custom_call" | custom-call | tf_op jit(solution)/shard_map/gla_layers/pallas_call | solution.py:515
  563.5 0.0 copy-start
  563.5 14.5 %copy.16 = bf16[1,2,2048,2048]{3,2,1,0:T(8,128)(2,1)} copy(bf16[1,2,2048,2048]{3,2,1,0:T(8,128)(2,1)} %bitcast.13) | data formatting | bytes 33554432
  578.0 0.0 copy-done
  578.0 2.0 copy.17
Async XLA Ops:
  563.5 14.5 %copy-start = (f32[2,1024,512]{2,1,0:T(8,128)S(1)}, f32[2,1024,512]{2,1,0:T(8,128)}, u32[]{:S(2)}) copy-start(f32[2,1024,512]{2,1,0:T(8,128)} %get-tuple-element.5) | copy-start | bytes 12582916
